TPU v7x, 256 devices: a whole 4x4x8 slice. The times are simulated.
256 devices in a mesh: batch: 32 (over x, z), mp: 8 (over y, core).
Axes of the slice: x: 4, y: 4, z: 8, core: 2. Of those that a mesh axis runs over, the one named last changes fastest.
Arguments:
- features: bfloat16 [4096, 65536], P('batch', 'mp'), may hold values from 0 to 4
- tiles: bfloat16 [2, 512, 3, 128, 128], P(None, 'mp', None, 'batch'), may hold values from -0.3125 to 0.3125
- biases: float32 [2, 65536], P(None, 'mp'), may hold values from -0.5 to 0
- in_block: int32 [2, 512, 3], replicated, may hold values from 0 to 511, as said below
Outputs:
- activations: bfloat16 [4096, 65536], P('batch', 'mp')
- row_means: float32 [4096], P('batch')
- grand: float32 [], replicated
Inputs may be any that keep to these rules, and one draw needn't show every extreme that they name: `in_block`: number the 192 tiles of mp shard m (column blocks m * 64 to (m + 1) * 64 - 1) in order of column block, then tile slot; tile number s reads a block of shard s // 24, that is an id in [(s // 24) * 64, (s // 24 + 1) * 64).
All inputs are finite; a program needn't handle non-finite values.
Results may differ from a plain program's by a relative error of at most 0.0052.
Values may be sent and summed in bfloat16 or wider, within the bound.
A program may use at most 128 MiB of HBM per device.

v0:
```python
import jax
import jax.numpy as jnp
from jax import lax
from jax.sharding import PartitionSpec as P

NEUR = 65536


def copy_for_each(x, axis):
    copies = jnp.broadcast_to(x, (lax.axis_size(axis), *x.shape))
    return lax.all_to_all(copies, axis, split_axis=0, concat_axis=0, tiled=True)


def of_everyone(x, axis):
    everything = copy_for_each(x, axis)
    return jnp.sum(everything, axis=0)


def on_device(features, tiles, biases, in_block):
    shard_count = lax.axis_size("mp")
    shard_self = lax.axis_index("mp")
    rows_here = features.shape[0]
    side = tiles.shape[4]
    cb_dev = features.shape[1] // side
    fan = tiles.shape[2]
    per_peer = cb_dev * fan // shard_count
    layer_total = tiles.shape[0]
    current = features
    for layer_no in range(layer_total):
        table = in_block[layer_no].reshape(shard_count, shard_count, per_peer)
        blocks_here = current.reshape(rows_here, cb_dev, side)
        wanted = (
            lax.dynamic_index_in_dim(table, shard_self, 1, False).reshape(-1) - shard_self * cb_dev
        )
        outgoing = jnp.take(blocks_here, wanted, axis=1)
        incoming = lax.all_to_all(outgoing, "mp", split_axis=1, concat_axis=1, tiled=True)
        inputs = incoming.reshape(rows_here, cb_dev, fan, side)
        layer_tiles = lax.all_gather(tiles[layer_no], "batch", axis=2, tiled=True)
        total = jnp.einsum(
            "rjki,jkio->rjo", inputs, layer_tiles, preferred_element_type=jnp.float32
        )
        shifted = total + biases[layer_no].reshape(cb_dev, side)[None, :, :]
        current = (
            jnp.clip(shifted, 0.0, 32.0).astype(jnp.bfloat16).reshape(rows_here, cb_dev * side)
        )
    partial_sum = jnp.sum(current.astype(jnp.float32), axis=1)
    row_means = of_everyone(partial_sum, "mp") / NEUR
    grand = of_everyone(jnp.sum(row_means), "batch") / (rows_here * lax.axis_size("batch"))
    return (current, row_means, grand)


def solution(mesh):
    placed = (P("batch", "mp"), P(None, "mp", None, "batch", None), P(None, "mp"), P())
    return jax.shard_map(
        on_device,
        mesh=mesh,
        in_specs=placed,
        out_specs=(P("batch", "mp"), P("batch"), P()),
        check_vma=False,
    )
```

profile of v0, /device:TPU:1, one launch (start us, length us, event | category | flops | bytes accessed | tf_op | source)
XLA Modules:
  0.0 264.9 jit_solution(18380495261153250147)
XLA Ops:
  7.2 0.0 copy-start.1
  7.2 0.0 all-gather.5.cloned.1.call-start
  7.2 1.2 fusion.20
  8.4 0.7 copy.62
  9.1 0.0 all-gather.5.cloned.1.call-update
  9.1 4.1 %copy.47 = bf16[128,8192]{0,1:T(8,128)(2,1)} copy(bf16[128,8192]{1,0:T(8,128)(2,1)} %param.6) | data formatting | bytes 4194304 | tf_op args[0]
  13.2 3.2 %copy.48 = bf16[128,64,128]{2,0,1:T(8,128)(2,1)S(1)} copy(bf16[128,64,128]{0,2,1:T(8,128)(2,1)} %bitcast.51) | data formatting | bytes 4194304 | tf_op jit(solution)/shard_map/reshape | solution.py:31
  16.4 0.0 copy-done.1
  16.5 0.1 copy.45
  16.6 0.1 reshape_squeeze.7
  16.8 0.1 copy.46
  16.9 0.1 reshape_squeeze.6
  17.1 0.1 sub.18
  17.2 8.0 %gather_fusion = bf16[192,128,128]{2,1,0:T(8,128)(2,1)} fusion(bf16[128,64,128]{2,0,1:T(8,128)(2,1)S(1)} %copy.48, s32[1024]{0:T(1024)S(1)} %pad_clamp_fusion.1), kind=kCustom, calls=%fused_computation.clone | custom fusion | bytes 12583680 | tf_op jit(solution)/shard_map/jit(_take)/gather | solution.py:35
  25.2 6.2 %select_bitcast_fusion.1 = bf16[128,192,128]{2,0,1:T(8,128)(2,1)} fusion(bf16[192,128,128]{2,1,0:T(8,128)(2,1)} %gather_fusion, pred[192]{0:T(512)(128)(4,1)S(1)} %compare_and_fusion.1), kind=kLoop, calls=%fused_computation.8 | loop fusion | flops 3145728 | bytes 12583104 | tf_op jit(solution)/shard_map/jit(_take)/select_n | solution.py:35
  31.4 0.0 copy-start
  31.4 7.9 %all-to-all-start = ((bf16[128,192,128]{2,0,1:T(8,128)(2,1)}), bf16[128,192,128]{2,0,1:T(8,128)(2,1)}, u32[]{:S(2)}, u32[]{:S(2)}) async-start(bf16[128,192,128]{2,0,1:T(8,128)(2,1)} %select_bitcast_fusion.1), calls=%async_computation | async-start | bytes 12582912 | tf_op jit(solution)/shard_map/all_to_all | solution.py:36
  39.3 0.0 all-gather.7.cloned.1.call-start
  39.3 0.7 copy.63
  40.0 0.0 all-gather.7.cloned.1.call-update
  40.0 0.1 sub.20
  40.1 0.0 copy-done
  40.2 0.1 fusion.21
  40.2 70.4 %all-to-all-done = bf16[128,192,128]{2,0,1:T(8,128)(2,1)} async-done(((bf16[128,192,128]{2,0,1:T(8,128)(2,1)}), bf16[128,192,128]{2,0,1:T(8,128)(2,1)}, u32[]{:S(2)}, u32[]{:S(2)}) %all-to-all-start) | async-done | bytes 6291488 | tf_op jit(solution)/shard_map/all_to_all | solution.py:36
  110.6 0.0 all-gather.5.cloned.1.call-done
  110.6 17.2 %fusion.13 = bf16[128,64,128]{2,0,1:T(8,128)(2,1)S(1)} fusion(f32[64,128]{1,0:T(8,128)S(1)} %bitcast.53, bf16[128,64,3,128]{3,0,2,1:T(8,128)(2,1)} %bitcast.2, bf16[1,64,3,128,128]{4,1,2,0,3:T(8,128)(2,1)} %all-gather.5.cloned.1.call-done), kind=kOutput, calls=%fused_computation.16 | convolution fusion | flops 808452096 | bytes 14712832 | tf_op jit(solution)/shard_map/rjki,jkio->rjo/dot_general | solution.py:39
  127.8 8.0 %gather_fusion.1 = bf16[192,128,128]{2,1,0:T(8,128)(2,1)} fusion(bf16[128,64,128]{2,0,1:T(8,128)(2,1)S(1)} %fusion.13, s32[1024]{0:T(1024)S(1)} %pad_clamp_fusion), kind=kCustom, calls=%fused_computation.1.clone | custom fusion | bytes 12583680 | tf_op jit(solution)/shard_map/jit(_take)/gather | solution.py:35
  135.8 6.0 %select_bitcast_fusion = bf16[128,192,128]{2,0,1:T(8,128)(2,1)} fusion(bf16[192,128,128]{2,1,0:T(8,128)(2,1)} %gather_fusion.1, pred[192]{0:T(512)(128)(4,1)S(1)} %compare_and_fusion), kind=kLoop, calls=%fused_computation.7 | loop fusion | flops 3145728 | bytes 12583104 | tf_op jit(solution)/shard_map/jit(_take)/select_n | solution.py:35
  141.8 5.6 %all-to-all-start.1 = ((bf16[128,192,128]{2,0,1:T(8,128)(2,1)}), bf16[128,192,128]{2,0,1:T(8,128)(2,1)}, u32[]{:S(2)}, u32[]{:S(2)}) async-start(bf16[128,192,128]{2,0,1:T(8,128)(2,1)} %select_bitcast_fusion), calls=%async_computation.1 | async-start | bytes 12582912 | tf_op jit(solution)/shard_map/all_to_all | solution.py:36
  147.4 42.6 %all-gather.7.cloned.1.call-done = bf16[1,64,3,128,128]{4,1,2,0,3:T(8,128)(2,1)} async-done(((bf16[1,64,3,4,128]{4,1,2,0,3:T(8,128)(2,1)}), bf16[1,64,3,128,128]{4,1,2,0,3:T(8,128)(2,1)}) %all-gather.7.cloned.1.call-update) | async-done | bytes 6291472 | tf_op jit(solution)/shard_map/all_gather | solution.py:38
  190.0 9.2 %copy.52 = bf16[1,64,3,128,128]{3,4,2,1,0:T(8,128)(2,1)} copy(bf16[1,64,3,128,128]{4,1,2,0,3:T(8,128)(2,1)} %all-gather.7.cloned.1.call-done) | data formatting | bytes 12582912 | tf_op jit(solution)/shard_map/all_gather | solution.py:38
  199.2 19.5 %all-to-all-done.1 = bf16[128,192,128]{2,0,1:T(8,128)(2,1)} async-done(((bf16[128,192,128]{2,0,1:T(8,128)(2,1)}), bf16[128,192,128]{2,0,1:T(8,128)(2,1)}, u32[]{:S(2)}, u32[]{:S(2)}) %all-to-all-start.1) | async-done | bytes 6291488 | tf_op jit(solution)/shard_map/all_to_all | solution.py:36
  218.7 8.6 %convert_reduce_fusion = (f32[128]{0:T(128)S(1)}, bf16[128,64,128]{2,0,1:T(8,128)(2,1)}) fusion(f32[64,128]{1,0:T(8,128)S(1)} %bitcast.52, bf16[128,64,3,128]{3,0,2,1:T(8,128)(2,1)} %bitcast.9, bf16[1,64,3,128,128]{3,4,2,1,0:T(8,128)(2,1)} %copy.52), kind=kOutput, calls=%fused_computation.15 | convolution fusion | flops 810549120 | bytes 14713344 | tf_op jit(solution)/shard_map/rjki,jkio->rjo/dot_general | solution.py:39
  227.3 7.9 %all_to_all.22 = f32[8,1,128]{2,1,0:T(1,128)S(1)} all-to-all(f32[8,1,128]{2,1,0:T(1,128)S(1)} %broadcast_in_dim.15), channel_id=1, replica_groups=mesh['batch'=32,'mp'=8] {'mp'}, dimensions={0} | all-to-all | bytes 8192 | tf_op jit(solution)/shard_map/all_to_all | solution.py:11
  235.2 1.1 fusion.19
  236.4 1.3 broadcast_in_dim.16
  237.6 9.3 %all-to-all-start.3 = ((f32[32,1,1]{2,1,0:T(1,128)}), f32[32,1,1]{2,1,0:T(1,128)S(1)}, u32[]{:S(2)}, u32[]{:S(2)}) async-start(f32[32,1,1]{2,1,0:T(1,128)} %broadcast_in_dim.16), calls=%async_computation.3 | async-start | bytes 32768 | tf_op jit(solution)/shard_map/all_to_all | solution.py:11
  247.0 3.2 %copy.54 = bf16[128,64,128]{0,2,1:T(8,128)(2,1)S(1)} copy(bf16[128,64,128]{2,0,1:T(8,128)(2,1)} %get-tuple-element.28) | data formatting | bytes 4194304 | tf_op jit(solution)/shard_map/convert_element_type | solution.py:44
  250.2 2.9 %copy.57 = bf16[128,8192]{1,0:T(8,128)(2,1)} copy(bf16[128,8192]{0,1:T(8,128)(2,1)S(1)} %bitcast.50) | data formatting | bytes 4194304
  253.1 2.5 all-to-all-done.3
  255.6 0.6 reduce_sum.39
  (10 shorter events, 0.1 us)
Async XLA Ops:
  7.2 9.3 %copy-start.1 = (s32[2,512,3]{1,0,2:T(2,128)S(1)}, s32[2,512,3]{1,0,2:T(2,128)}, u32[]{:S(2)}) copy-start(s32[2,512,3]{1,0,2:T(2,128)} %param.9) | copy-start | bytes 36868
  7.2 103.4 %all-gather.5.cloned.1.call-start = ((), (), s32[]{:S(2)}) async-start(), calls=%async_computation.4 | async-start | bytes 6488064 | tf_op jit(solution)/shard_map/all_gather | solution.py:38
  31.4 8.8 %copy-start = (f32[2,8192]{1,0:T(2,128)S(1)}, f32[2,8192]{1,0:T(2,128)}, u32[]{:S(2)}) copy-start(f32[2,8192]{1,0:T(2,128)} %param.8) | copy-start | bytes 196612
  31.4 79.2 %all-to-all-start = ((bf16[128,192,128]{2,0,1:T(8,128)(2,1)}), bf16[128,192,128]{2,0,1:T(8,128)(2,1)}, u32[]{:S(2)}, u32[]{:S(2)}) async-start(bf16[128,192,128]{2,0,1:T(8,128)(2,1)} %select_bitcast_fusion.1), calls=%async_computation | async-start | bytes 12582912 | tf_op jit(solution)/shard_map/all_to_all | solution.py:36
  39.3 150.7 %all-gather.7.cloned.1.call-start = ((), (), s32[]{:S(2)}) async-start(), calls=%async_computation.5 | async-start | bytes 6488064 | tf_op jit(solution)/shard_map/all_gather | solution.py:38
  141.8 76.9 %all-to-all-start.1 = ((bf16[128,192,128]{2,0,1:T(8,128)(2,1)}), bf16[128,192,128]{2,0,1:T(8,128)(2,1)}, u32[]{:S(2)}, u32[]{:S(2)}) async-start(bf16[128,192,128]{2,0,1:T(8,128)(2,1)} %select_bitcast_fusion), calls=%async_computation.1 | async-start | bytes 12582912 | tf_op jit(solution)/shard_map/all_to_all | solution.py:36
  237.6 18.0 %all-to-all-start.3 = ((f32[32,1,1]{2,1,0:T(1,128)}), f32[32,1,1]{2,1,0:T(1,128)S(1)}, u32[]{:S(2)}, u32[]{:S(2)}) async-start(f32[32,1,1]{2,1,0:T(1,128)} %broadcast_in_dim.16), calls=%async_computation.3 | async-start | bytes 32768 | tf_op jit(solution)/shard_map/all_to_all | solution.py:11
Sparse Core Ops, SparseCore 0:
  10.6 91.0 all-gather.4
  104.8 85.1 all-gather.6
where the time goes:
time: 266 us; the launch traced here: 265 us
  waiting for transfers between devices  135 us (51%)
  local copies, waits for them, and re-layouts  43.2 us (16%)
  matrix products  25.8 us (10%)
  starting transfers between devices  22.9 us (9%)
  between operations  16 us (6%)
  other arithmetic  14.1 us (5%)
  blocking collectives  7.91 us (3%)
    all_to_all x2, waiting for transfers between devices, on_device(): lax.all_to_all(outgoing, 'mp', split_axis=1, concat_axis=1, tiled=True)  89.9 us
    all_gather x2, waiting for transfers between devices, on_device(): layer_tiles = lax.all_gather(tiles[layer_no], 'batch', axis=2, tiled=True)  42.6 us
    dot_general x2, matrix products, on_device(): jnp.einsum('rjki,jkio->rjo', inputs, layer_tiles, preferred_element_type=...  25.8 us
    gather x2, local copies, waits for them, and re-layouts, on_device(): outgoing = jnp.take(blocks_here, wanted, axis=1)  16 us
    all_to_all x2, starting transfers between devices, on_device(): lax.all_to_all(outgoing, 'mp', split_axis=1, concat_axis=1, tiled=True)  13.5 us
    select_n x4, other arithmetic, on_device(): outgoing = jnp.take(blocks_here, wanted, axis=1)  12.2 us
    all_to_all x1, starting transfers between devices, copy_for_each(): return lax.all_to_all(copies, axis, split_axis=0, concat_axis=0, tiled=True)  9.34 us
    all_gather x1, local copies, waits for them, and re-layouts, on_device(): layer_tiles = lax.all_gather(tiles[layer_no], 'batch', axis=2, tiled=True)  9.18 us
  transfers between devices with their start and end apart: 5, of which 4 were waited for; matrix products, arithmetic and copies ran while one was open for 26% of the time, Pallas kernels for 0%

commit v1 on v0

v1 whole, which is shorter than its diff:
```python
import functools

import jax
import jax.numpy as jnp
from jax import lax
from jax.experimental import pallas as pl
from jax.experimental.pallas import tpu as pltpu
from jax.sharding import PartitionSpec as P

MESH = pl.DeviceIdType.MESH
NX, NZ = 4, 8
NY, NC = 4, 2
TA = 10
LAG = 1
STAGES = 6
FAR_FIRST = ((2, 0), (2, 1), (1, 0), (3, 0), (1, 1), (3, 1), (0, 1), (0, 0))
SELF_FIRST = ((0, 0),) + FAR_FIRST[:-1]
F32 = jnp.float32
BF16 = jnp.bfloat16


def pick(j, values):
    total = 0
    for i, v in enumerate(values):
        total = total + jnp.where(j == i, v, 0)
    return total


def kernel(
    neur, rows_all,
    ib, feat, tiles, bias,
    out, means, grand,
    X0, X1, WA, WB, B, O0, O1, acc, RS, GX, GZ,
    p0s, p0r, pbs, pbr, sA, rA, sB, rB, ys, yr, rss, rsr, gxs, gxr, gzs, gzr, fsem,
):
    layers = tiles.shape[0]
    shards = tiles.shape[1]
    per_chunk = tiles.shape[2]
    cols = per_chunk // 3
    blocks = cols * shards
    chunks = layers * shards
    b = lax.axis_index("batch")
    me = lax.axis_index("mp")
    x, z = b // NZ, b % NZ
    y, c = me // NC, me % NC
    xr, xl = (x + 1) % NX, (x + NX - 1) % NX

    def zat(d):
        return (z + d + NZ) % NZ

    def at(xx, zz):
        return {"batch": xx * NZ + zz}

    right, left = at(xr, z), at(xl, z)
    up, down = at(x, zat(1)), at(x, zat(-1))

    def peer(dy, dc):
        return ((y + dy) % NY) * NC + (c + dc) % NC

    mp_peers = [peer(dy, dc) for dy, dc in FAR_FIRST[:-1]]

    def remote(src, dst, ss, rs, dev):
        return pltpu.make_async_remote_copy(
            src_ref=src, dst_ref=dst, send_sem=ss, recv_sem=rs, device_id=dev, device_id_type=MESH
        )

    def load(j, _):
        at_j = pl.ds(pl.multiple_of(j * 128, 128), 128)
        pltpu.make_async_copy(feat.at[:, at_j], X0.at[j], fsem).start()
        return 0

    barrier = pltpu.get_barrier_semaphore()
    count = 0
    for s in mp_peers:
        pl.semaphore_signal(barrier, inc=1, device_id={"mp": s}, device_id_type=MESH)
        count += 1
    for d in range(1, NX):
        pl.semaphore_signal(
            barrier, inc=1, device_id=at((x + d) % NX, z), device_id_type=MESH
        )
        count += 1
    for d in range(1, NZ):
        pl.semaphore_signal(barrier, inc=1, device_id=at(x, zat(d)), device_id_type=MESH)
        count += 1
    own = []
    for l in range(layers):
        q = l * shards + me
        own.append(
            pltpu.make_async_copy(tiles.at[l, me, 0:TA], WA.at[q, z, x], p0r.at[q, 0])
        )
        own.append(
            pltpu.make_async_copy(tiles.at[l, me, TA:per_chunk], WB.at[q, x, z], p0r.at[q, 1])
        )
    own.append(
        pltpu.make_async_copy(
            bias.at[:, pl.ds(pl.multiple_of(me * cols * 128, 128), cols * 128)],
            B.at[me],
            pbr.at[me],
        )
    )
    for copy in own:
        copy.start()
    lax.fori_loop(0, blocks, load, 0)
    pl.semaphore_wait(barrier, count)

    def part_a(l, i, s):
        q = l * shards + me
        return remote(
            tiles.at[l, s, 0:TA], WA.at[q, z, x], p0s.at[l, i, 0], p0r.at[q, 0], {"mp": s}
        )

    def part_b(l, i, s):
        q = l * shards + me
        return remote(
            tiles.at[l, s, TA:per_chunk], WB.at[q, x, z], p0s.at[l, i, 1], p0r.at[q, 1], {"mp": s}
        )

    def bias_to(i, s):
        cut = pl.ds(pl.multiple_of(s * cols * 128, 128), cols * 128)
        return remote(bias.at[:, cut], B.at[me], pbs.at[i], pbr.at[me], {"mp": s})

    order = [peer(NY - dy, dc) for dy, dc in FAR_FIRST[:-1]]
    for l in range(layers):
        for i, s in enumerate(order):
            part_a(l, i, s).start()
            part_b(l, i, s).start()
        if l == 0:
            for i, s in enumerate(order):
                bias_to(i, s).start()

    acc[...] = jnp.zeros_like(acc)

    def owner(k):
        l, j = k // shards, k % shards
        dy = jnp.where(
            l == layers - 1,
            pick(j, [d for d, _ in FAR_FIRST]),
            pick(j, [d for d, _ in SELF_FIRST]),
        )
        dc = jnp.where(
            l == layers - 1,
            pick(j, [d for _, d in FAR_FIRST]),
            pick(j, [d for _, d in SELF_FIRST]),
        )
        return l, peer(dy, dc)

    def a_copies(q, e):
        def go(ref, i, dev):
            return lambda: remote(ref, ref, sA.at[q, i], rA.at[q, i], dev)

        far_x = xl * (1 - e) + xr * e
        far_z = zat(-3) * (1 - e) + zat(3) * e
        to_x = at(xr * (1 - e) + xl * e, z)
        to_z = at(x, zat(1) * (1 - e) + zat(-1) * e)
        return [
            go(WA.at[q, z, x], 0, right),
            go(WA.at[q, z, x], 1, left),
            go(WA.at[q, z, far_x], 2, to_x),
            go(WA.at[q, z], 3, up),
            go(WA.at[q, z], 4, down),
            go(WA.at[q, zat(-1)], 5, up),
            go(WA.at[q, zat(1)], 6, down),
            go(WA.at[q, zat(-2)], 7, up),
            go(WA.at[q, zat(2)], 8, down),
            go(WA.at[q, far_z], 9, to_z),
        ]

    def b_copies(q, e):
        def go(ref, i, dev):
            return lambda: remote(ref, ref, sB.at[q, i], rB.at[q, i], dev)

        far_x = xl * (1 - e) + xr * e
        far_z = zat(3) * (1 - e) + zat(-3) * e
        to_x = at(xr * (1 - e) + xl * e, z)
        to_z = at(x, zat(-1) * (1 - e) + zat(1) * e)
        return [
            go(WB.at[q, x, z], 0, up),
            go(WB.at[q, x, z], 1, down),
            go(WB.at[q, x, zat(-1)], 2, up),
            go(WB.at[q, x, zat(1)], 3, down),
            go(WB.at[q, x, zat(-2)], 4, up),
            go(WB.at[q, x, zat(2)], 5, down),
            go(WB.at[q, x, far_z], 6, to_z),
            go(WB.at[q, x], 7, right),
            go(WB.at[q, x], 8, left),
            go(WB.at[q, far_x], 9, to_x),
        ]


    def stage(h, k):
        l, m = owner(k)
        q = l * shards + m
        e = k % 2
        a, bb = a_copies(q, e), b_copies(q, e)
        if h == 0:
            pltpu.make_async_copy(WA.at[q, z, x], WA.at[q, z, x], p0r.at[q, 0]).wait()
            a[0]().start()
            a[1]().start()
            pltpu.make_async_copy(WB.at[q, x, z], WB.at[q, x, z], p0r.at[q, 1]).wait()
            bb[0]().start()
            bb[1]().start()
        elif h == 1:
            a[0]().wait_recv()
            a[1]().wait_recv()
            a[2]().start()
            bb[0]().wait_recv()
            bb[2]().start()
            bb[1]().wait_recv()
            bb[3]().start()
        elif h == 2:
            a[2]().wait_recv()
            a[3]().start()
            a[4]().start()
            bb[2]().wait_recv()
            bb[4]().start()
            bb[3]().wait_recv()
            bb[5]().start()
        elif h == 3:
            a[3]().wait_recv()
            a[5]().start()
            a[4]().wait_recv()
            a[6]().start()
            bb[4]().wait_recv()
            bb[5]().wait_recv()
            bb[6]().start()
        elif h == 4:
            a[5]().wait_recv()
            a[7]().start()
            a[6]().wait_recv()
            a[8]().start()
            bb[6]().wait_recv()
            bb[7]().start()
            bb[8]().start()
        elif h == 5:
            a[7]().wait_recv()
            a[8]().wait_recv()
            a[9]().start()
            bb[7]().wait_recv()
            bb[8]().wait_recv()
            bb[9]().start()
        else:
            a[9]().wait_recv()
            bb[9]().wait_recv()

    mine = pl.ds(me * cols, cols)
    mine_out = pl.ds(pl.multiple_of(me * cols * 128, 128), cols * 128)

    def y_copy(l, m):
        if l == 0:
            src, dst = O0.at[m], X1.at[mine]
        else:
            src, dst = O1.at[m], out.at[:, mine_out]
        return remote(src, dst, ys.at[l, m], yr.at[l, me], {"mp": m})

    def y_arrival(l, s):
        if l == 0:
            src, dst = O0.at[s], X1.at[pl.ds(s * cols, cols)]
        else:
            cut = pl.ds(pl.multiple_of(s * cols * 128, 128), cols * 128)
            src, dst = O1.at[s], out.at[:, cut]
        remote(src, dst, ys.at[l, s], yr.at[l, s], {"mp": s}).wait_recv()

    def compute(l, k):
        _, m = owner(k)
        q = l * shards + m
        source = X0 if l == 0 else X1
        if l == 0:

            @pl.when(k == 0)
            def _():
                pltpu.make_async_copy(X0, X0, fsem).wait()

            pltpu.make_async_copy(B.at[m], B.at[m], pbr.at[m]).wait()
        else:

            @pl.when(k == shards)
            def _():
                for s in mp_peers:
                    y_arrival(0, s)

        for j in range(cols):
            total = None
            for t in range(3):
                f = 3 * j + t
                block = lax.rem(ib[t, l, m * blocks + me * cols + j], blocks)
                lhs = source[block]
                if f < TA:
                    w = jnp.transpose(WA[q, :, :, f], (1, 0, 2, 3)).reshape(128, 128)
                else:
                    w = WB[q, :, :, f - TA].reshape(128, 128)
                d = jnp.dot(lhs, w, preferred_element_type=F32)
                total = d if total is None else total + d
            row = B[m, l : l + 1, j * 128 : (j + 1) * 128]
            value = jnp.clip(total + row, 0.0, 32.0).astype(BF16)
            if l == 0:
                O0[m, j] = value
            else:
                O1[m, :, j * 128 : (j + 1) * 128] = value
                acc[...] += value.astype(F32)

        @pl.when(m == me)
        def _():
            if l == 0:
                X1[mine] = O0[m]
            else:
                out[:, mine_out] = O1[m]

        @pl.when(m != me)
        def _():
            y_copy(l, m).start()

    def step(i, _):
        for h in range(STAGES, -1, -1):
            k = i - h

            @pl.when(jnp.logical_and(k >= 0, k < chunks))
            def _():
                stage(h, k)

        first = i - STAGES

        @pl.when(jnp.logical_and(first >= 0, first < shards))
        def _():
            compute(0, first)

        second = first - LAG

        @pl.when(second >= shards)
        def _():
            compute(1, second)

        return 0

    lax.fori_loop(0, chunks + STAGES + LAG, step, 0)

    part = jnp.sum(acc[...].T, axis=0, keepdims=True)
    RS[me] = jnp.broadcast_to(part, (8, 128))
    rs_copies = [
        remote(RS.at[me], RS.at[me], rss.at[i], rsr.at[me], {"mp": s})
        for i, s in enumerate(mp_peers)
    ]
    for copy in rs_copies:
        copy.start()

    for i, s in enumerate(mp_peers):
        remote(RS.at[s], RS.at[s], rss.at[i], rsr.at[s], {"mp": s}).wait_recv()
    row = RS[0, 0:1]
    for s in range(1, shards):
        row = row + RS[s, 0:1]
    row = row / neur
    means[...] = row
    GX[x] = jnp.broadcast_to(jnp.sum(row, axis=1, keepdims=True), (8, 128))
    gx_copies = [
        remote(GX.at[x], GX.at[x], gxs.at[d], gxr.at[x], at((x + d) % NX, z))
        for d in range(1, NX)
    ]
    for copy in gx_copies:
        copy.start()
    for d in range(1, NX):
        n = (x + d) % NX
        remote(GX.at[n], GX.at[n], gxs.at[d], gxr.at[n], at(n, z)).wait_recv()
    GZ[z] = GX[0] + GX[1] + GX[2] + GX[3]
    gz_copies = [
        remote(GZ.at[z], GZ.at[z], gzs.at[d], gzr.at[z], at(x, zat(d))) for d in range(1, NZ)
    ]
    for copy in gz_copies:
        copy.start()
    for d in range(1, NZ):
        n = zat(d)
        remote(GZ.at[n], GZ.at[n], gzs.at[d], gzr.at[n], at(x, n)).wait_recv()
    total = GZ[0, 0:1]
    for n in range(1, NZ):
        total = total + GZ[n, 0:1]
    grand[...] = total / rows_all

    for s in mp_peers:
        y_arrival(1, s)

    def drain(k, _):
        for copy in a_copies(k, 0) + b_copies(k, 0):
            copy().wait_send()
        return 0

    lax.fori_loop(0, chunks, drain, 0)
    for l in range(layers):
        for i, s in enumerate(order):
            part_a(l, i, s).wait_send()
            part_b(l, i, s).wait_send()
        for s in mp_peers:
            y_copy(l, s).wait_send()
    for i, s in enumerate(order):
        bias_to(i, s).wait_send()
    for copy in rs_copies + gx_copies + gz_copies:
        copy.wait_send()


def on_device(features, tiles, biases, in_block):
    layers, cb, fan, own_rows, side = tiles.shape
    rows = features.shape[0]
    shards = lax.axis_size("mp")
    groups = lax.axis_size("batch")
    per_chunk = cb // shards * fan
    chunks = layers * shards
    vmem = pl.BlockSpec(memory_space=pltpu.VMEM)
    any_ = pl.BlockSpec(memory_space=pl.ANY)
    dma = pltpu.SemaphoreType.DMA
    current, means, grand = pl.pallas_call(
        functools.partial(kernel, cb * shards * side, rows * groups),
        out_shape=(
            jax.ShapeDtypeStruct((rows, cb * side), BF16),
            jax.ShapeDtypeStruct((1, rows), F32),
            jax.ShapeDtypeStruct((1, 128), F32),
        ),
        in_specs=[pl.BlockSpec(memory_space=pltpu.SMEM), any_, vmem, vmem],
        out_specs=(vmem, vmem, vmem),
        scratch_shapes=[
            pltpu.VMEM((cb, rows, side), BF16),
            pltpu.VMEM((cb, rows, side), BF16),
            pltpu.VMEM((chunks, NZ, NX, TA, own_rows, side), BF16),
            pltpu.VMEM((chunks, NX, NZ, per_chunk - TA, own_rows, side), BF16),
            pltpu.VMEM((shards, layers, cb // shards * side), F32),
            pltpu.VMEM((shards, cb // shards, rows, side), BF16),
            pltpu.VMEM((shards, rows, cb // shards * side), BF16),
            pltpu.VMEM((rows, side), F32),
            pltpu.VMEM((shards, 8, 128), F32),
            pltpu.VMEM((NX, 8, 128), F32),
            pltpu.VMEM((NZ, 8, 128), F32),
            dma((layers, shards - 1, 2)),
            dma((chunks, 2)),
            dma((shards - 1,)),
            dma((shards,)),
            dma((chunks, 10)),
            dma((chunks, 10)),
            dma((chunks, 10)),
            dma((chunks, 10)),
            dma((layers, shards)),
            dma((layers, shards)),
            dma((shards - 1,)),
            dma((shards,)),
            dma((NX,)),
            dma((NX,)),
            dma((NZ,)),
            dma((NZ,)),
            dma,
        ],
        compiler_params=pltpu.CompilerParams(
            collective_id=0, has_side_effects=True, vmem_limit_bytes=48 * 1024 * 1024
        ),
    )(
        jnp.transpose(in_block, (2, 0, 1)),
        features,
        tiles.reshape(layers, shards, per_chunk, own_rows, side),
        biases,
    )
    return current, means.reshape(rows), grand[0, 0]


def solution(mesh):
    placed = (P("batch", "mp"), P(None, "mp", None, "batch", None), P(None, "mp"), P())
    return jax.shard_map(
        on_device,
        mesh=mesh,
        in_specs=placed,
        out_specs=(P("batch", "mp"), P("batch"), P()),
        check_vma=False,
    )
```

time: 266 us -> 150 us (0.56)
  Pallas kernels: 0 us -> 142 us
  waiting for transfers between devices: 135 us -> 0 us
  local copies, waits for them, and re-layouts: 43.2 us -> 5.96 us
  matrix products: 25.8 us -> 0 us
  starting transfers between devices: 22.9 us -> 0 us
  between operations: 16 us -> 1.82 us
  other arithmetic: 14.1 us -> 0 us
  blocking collectives: 7.91 us -> 0 us
    pallas_call x0 -> x1, Pallas kernels: none -> 142 us  [on_device(): pl.pallas_call(functools.partial(kernel, cb * shards * side, rows * group...]
    all_to_all x3 -> x0, waiting for transfers between devices: 92.4 us -> none  [the longest x2 89.9 us: on_device(): lax.all_to_all(outgoing, 'mp', split_axis=1, concat_axis=1, tiled=True)]
    all_gather x2 -> x0, waiting for transfers between devices: 42.6 us -> none  [on_device(): layer_tiles = lax.all_gather(tiles[layer_no], 'batch', axis=2, tiled=True)]
    dot_general x2 -> x0, matrix products: 25.8 us -> none  [on_device(): jnp.einsum('rjki,jkio->rjo', inputs, layer_tiles, preferred_element_type=...]
    all_to_all x3 -> x0, starting transfers between devices: 22.9 us -> none  [the longest x2 13.5 us: on_device(): lax.all_to_all(outgoing, 'mp', split_axis=1, concat_axis=1, tiled=True)]
    gather x2 -> x0, local copies, waits for them, and re-layouts: 16 us -> none  [on_device(): outgoing = jnp.take(blocks_here, wanted, axis=1)]
    select_n x4 -> x0, other arithmetic: 12.2 us -> none  [on_device(): outgoing = jnp.take(blocks_here, wanted, axis=1)]
    all_gather x1 -> x0, local copies, waits for them, and re-layouts: 9.18 us -> none  [on_device(): layer_tiles = lax.all_gather(tiles[layer_no], 'batch', axis=2, tiled=True)]
  transfers between devices with their start and end apart: 5 -> 0, of which waited for: 4 -> 0; matrix products, arithmetic and copies ran while one was open for 26% -> 0% of each run, Pallas kernels for 0% -> 0%
where the time goes in v1:
time: 150 us
  Pallas kernels  142 us (95%)
  local copies, waits for them, and re-layouts  5.96 us (4%)
  between operations  1.82 us (1%)
    pallas_call x1, Pallas kernels, on_device(): pl.pallas_call(functools.partial(kernel, cb * shards * side, rows * group...  142 us
    unnamed x10, local copies, waits for them, and re-layouts  5.96 us

profile of v1, /device:TPU:1, one launch (start us, length us, event | category | flops | bytes accessed | tf_op | source)
XLA Modules:
  0.0 149.6 jit_solution(16738390333293984114)
XLA Ops:
  0.6 0.0 copy-start
  0.6 1.6 %copy-done = bf16[128,8192]{1,0:T(8,128)(2,1)S(1)} copy-done((bf16[128,8192]{1,0:T(8,128)(2,1)S(1)}, bf16[128,8192]{1,0:T(8,128)(2,1)}, u32[]{:S(2)}) %copy-start) | copy-done | bytes 2097176
  2.2 0.0 copy-start.1
  2.2 1.0 copy-done.1
  3.2 0.0 copy-start.2
  3.2 0.8 copy-done.2
  4.1 0.0 copy-start.3
  4.1 0.7 copy-done.3
  4.8 141.8 %shard_map.67 = (bf16[128,8192]{1,0:T(8,128)(2,1)S(1)}, f32[1,128]{1,0:T(1,128)S(1)}, f32[1,128]{1,0:T(1,128)S(1)}) custom-call(s32[3,2,512]{2,1,0:T(2,128)S(1)} %bitcast.6, bf16[128,8192]{1,0:T(8,128)(2,1)S(1)} %copy-done, bf16[2,8,24,4,128]{4,3,2,1,0:T(4,128)(2,1)S(1)} %bitcast.5, f32[2,8192]{1,0:T(2,128)S(1)} %copy-done.2), custom_call_target="tpu_custom_call" | custom-call | tf_op jit(solution)/shard_map/pallas_call | solution.py:407
  146.6 1.3 copy.10
  147.9 0.5 copy.11
Async XLA Ops:
  0.6 1.6 %copy-start = (bf16[128,8192]{1,0:T(8,128)(2,1)S(1)}, bf16[128,8192]{1,0:T(8,128)(2,1)}, u32[]{:S(2)}) copy-start(bf16[128,8192]{1,0:T(8,128)(2,1)} %feat.1) | copy-start | bytes 6291460
  2.2 1.0 copy-start.1
  3.2 0.8 copy-start.2
  4.1 0.7 copy-start.3

commit v2 on v1

v2 whole, which is shorter than its diff:
```python
import functools

import jax
import jax.numpy as jnp
from jax import lax
from jax.experimental import pallas as pl
from jax.experimental.pallas import tpu as pltpu
from jax.sharding import PartitionSpec as P

NX, NZ = 4, 8
NY, NC = 4, 2
TA = 10
LAGS_A = (0, 1, 2, 3, 4, 5, 6)
LAGS_B = (0, 1, 2, 3, 4, 5, 6)
LAG = 1
F32 = jnp.float32
BF16 = jnp.bfloat16


def kernel(
    neur, rows_all,
    ib, feat, tiles, bias,
    out, means, grand,
    X0, X1, WA, WB, B, O0, O1, acc, RS, G, ids,
    p0s, p0r, pbs, pbr, sA, rA, sB, rB, ys, yr, rss, rsr, gs, gr, fsem, isem,
):
    layers = tiles.shape[0]
    shards = tiles.shape[1]
    per_chunk = tiles.shape[2]
    cols = per_chunk // 3
    blocks = cols * shards
    chunks = layers * shards
    b = lax.axis_index("batch")
    me = lax.axis_index("mp")
    x, z = b // NZ, b % NZ
    y, c = me // NC, me % NC
    xr, xl = (x + 1) % NX, (x + NX - 1) % NX

    def zat(d):
        return (z + d + NZ) % NZ

    def device(xx, zz, s):
        return (xx * NZ + zz) * shards + s

    near = {d: zat(d) for d in range(-3, 4)}
    right, left = device(xr, z, me), device(xl, z, me)
    up, down = device(x, near[1], me), device(x, near[-1], me)

    def peer(dy, dc):
        return lax.rem(y + dy, NY) * NC + lax.rem(c + dc, NC)

    def mate(s):
        return device(x, z, s)

    offsets = [(2, 0), (2, 1), (1, 0), (3, 0), (1, 1), (3, 1), (0, 1)]
    mp_peers = [peer(dy, dc) for dy, dc in offsets]

    def remote(src, dst, ss, rs, dev):
        return pltpu.make_async_remote_copy(
            src_ref=src,
            dst_ref=dst,
            send_sem=ss,
            recv_sem=rs,
            device_id=dev,
            device_id_type=pl.DeviceIdType.LOGICAL,
        )

    def load(j, _):
        at_j = pl.ds(pl.multiple_of(j * 128, 128), 128)
        pltpu.make_async_copy(feat.at[:, at_j], X0.at[j], fsem).start()
        return 0

    barrier = pltpu.get_barrier_semaphore()
    greeted = [mate(s) for s in mp_peers] + [right, left, up, down]
    for dev in greeted:
        pl.semaphore_signal(
            barrier, inc=1, device_id=dev, device_id_type=pl.DeviceIdType.LOGICAL
        )
    own = []
    for l in range(layers):
        q = l * shards + me
        own.append(
            pltpu.make_async_copy(tiles.at[l, me, 0:TA], WA.at[q, z, x], p0r.at[q, 0])
        )
        own.append(
            pltpu.make_async_copy(tiles.at[l, me, TA:per_chunk], WB.at[q, x, z], p0r.at[q, 1])
        )
    own.append(
        pltpu.make_async_copy(
            bias.at[:, pl.ds(pl.multiple_of(me * cols * 128, 128), cols * 128)],
            B.at[me],
            pbr.at[me],
        )
    )
    for copy in own:
        copy.start()
    pltpu.make_async_copy(ib, ids, isem).start()
    lax.fori_loop(0, blocks, load, 0)
    pl.semaphore_wait(barrier, len(greeted))

    def part_a(l, i, s):
        q = l * shards + me
        return remote(
            tiles.at[l, s, 0:TA], WA.at[q, z, x], p0s.at[l, i, 0], p0r.at[q, 0], mate(s)
        )

    def part_b(l, i, s):
        q = l * shards + me
        return remote(
            tiles.at[l, s, TA:per_chunk], WB.at[q, x, z], p0s.at[l, i, 1], p0r.at[q, 1], mate(s)
        )

    def bias_to(i, s):
        cut = pl.ds(pl.multiple_of(s * cols * 128, 128), cols * 128)
        return remote(bias.at[:, cut], B.at[me], pbs.at[i], pbr.at[me], mate(s))

    order = [peer(NY - dy, dc) for dy, dc in offsets]
    for l in range(layers):
        for i in range(shards - 1):
            part_a(l, i, order[i]).start()
            part_b(l, i, order[i]).start()
        if l == 0:
            for i, s in enumerate(order):
                bias_to(i, s).start()

    acc[...] = jnp.zeros_like(acc)

    def owner(k):
        l = jnp.where(k >= shards, 1, 0)
        n = lax.rem(k + (1 - l) * (shards - 1), shards)
        dy = jnp.where(n < 2, 2, jnp.where(n < 6, 1 + 2 * lax.rem(n, 2), 0))
        dc = jnp.where(n < 2, n, jnp.where(n < 6, lax.div(n - 2, 2), 7 - n))
        return l, peer(dy, dc)

    def a_copies(q):
        def go(ref, i, dev):
            return lambda: remote(ref, ref, sA.at[q, i], rA.at[q, i], dev)

        half, cut = NX // 2, TA // 2
        return [
            go(WA.at[q, z, x], 0, right),
            go(WA.at[q, z, x], 1, left),
            go(WA.at[q, z, xl, 0:cut], 2, right),
            go(WA.at[q, z, xr, cut:TA], 3, left),
            go(WA.at[q, z], 4, up),
            go(WA.at[q, z], 5, down),
            go(WA.at[q, near[-1]], 6, up),
            go(WA.at[q, near[1]], 7, down),
            go(WA.at[q, near[-2]], 8, up),
            go(WA.at[q, near[2]], 9, down),
            go(WA.at[q, near[-3], 0:half], 10, up),
            go(WA.at[q, near[3], half:NX], 11, down),
        ]

    def b_copies(q):
        def go(ref, i, dev):
            return lambda: remote(ref, ref, sB.at[q, i], rB.at[q, i], dev)

        tb = per_chunk - TA
        half, cut = NZ // 2, tb // 2
        return [
            go(WB.at[q, x, z], 0, up),
            go(WB.at[q, x, z], 1, down),
            go(WB.at[q, x, near[-1]], 2, up),
            go(WB.at[q, x, near[1]], 3, down),
            go(WB.at[q, x, near[-2]], 4, up),
            go(WB.at[q, x, near[2]], 5, down),
            go(WB.at[q, x, near[-3], 0:cut], 6, up),
            go(WB.at[q, x, near[3], cut:tb], 7, down),
            go(WB.at[q, x], 8, right),
            go(WB.at[q, x], 9, left),
            go(WB.at[q, xl, 0:half], 10, right),
            go(WB.at[q, xr, half:NZ], 11, left),
        ]

    def stage_a(h, q):
        copies = a_copies(q)

        def forward(needs, starts):
            for n in needs:
                copies[n]().wait_recv()
            for n in starts:
                copies[n]().start()

        if h == 0:
            pltpu.make_async_copy(WA.at[q, z, x], WA.at[q, z, x], p0r.at[q, 0]).wait()
            forward((), (0, 1))
        elif h == 1:
            forward((0,), (2,))
            forward((1,), (3,))
        elif h == 2:
            forward((2, 3), (4, 5))
        elif h < 6:
            forward((2 * h - 2,), (2 * h,))
            forward((2 * h - 1,), (2 * h + 1,))
        else:
            forward((10, 11), ())

    def stage_b(h, q):
        copies = b_copies(q)

        def forward(needs, starts):
            for n in needs:
                copies[n]().wait_recv()
            for n in starts:
                copies[n]().start()

        if h == 0:
            pltpu.make_async_copy(WB.at[q, x, z], WB.at[q, x, z], p0r.at[q, 1]).wait()
            forward((), (0, 1))
        elif h == 4:
            forward((6, 7), (8, 9))
        elif h < 6:
            forward((2 * h - 2,), (2 * h,))
            forward((2 * h - 1,), (2 * h + 1,))
        else:
            forward((10, 11), ())

    mine = pl.ds(me * cols, cols)
    mine_out = pl.ds(pl.multiple_of(me * cols * 128, 128), cols * 128)

    def y_copy(l, m):
        if l == 0:
            src, dst = O0.at[m], X1.at[mine]
        else:
            src, dst = O1.at[m], out.at[:, mine_out]
        return remote(src, dst, ys.at[l, m], yr.at[l, me], mate(m))

    def y_arrival(l, s):
        if l == 0:
            src, dst = O0.at[s], X1.at[pl.ds(s * cols, cols)]
        else:
            cut = pl.ds(pl.multiple_of(s * cols * 128, 128), cols * 128)
            src, dst = O1.at[s], out.at[:, cut]
        remote(src, dst, ys.at[l, s], yr.at[l, s], mate(s)).wait_recv()

    def compute(l, k):
        _, m = owner(k)
        q = l * shards + m
        source = X0 if l == 0 else X1
        if l == 0:

            @pl.when(k == 0)
            def _():
                pltpu.make_async_copy(X0, X0, fsem).wait()
                pltpu.make_async_copy(ib, ids, isem).wait()

            pltpu.make_async_copy(B.at[m], B.at[m], pbr.at[m]).wait()
        else:

            @pl.when(k == shards)
            def _():
                for s in mp_peers:
                    y_arrival(0, s)

        for j in range(cols):
            total = None
            for t in range(3):
                f = 3 * j + t
                block = lax.rem(ids[t, l, m * blocks + me * cols + j], blocks)
                lhs = source[block]
                if f < TA:
                    w = jnp.transpose(WA[q, :, :, f], (1, 0, 2, 3)).reshape(128, 128)
                else:
                    w = WB[q, :, :, f - TA].reshape(128, 128)
                d = jnp.dot(lhs, w, preferred_element_type=F32)
                total = d if total is None else total + d
            row = B[m, l : l + 1, j * 128 : (j + 1) * 128]
            value = jnp.clip(total + row, 0.0, 32.0).astype(BF16)
            if l == 0:
                O0[m, j] = value
            else:
                O1[m, :, j * 128 : (j + 1) * 128] = value
                acc[...] += value.astype(F32)

        @pl.when(m == me)
        def _():
            if l == 0:
                X1[mine] = O0[m]
            else:
                out[:, mine_out] = O1[m]

        @pl.when(m != me)
        def _():
            y_copy(l, m).start()

    def ring_steps(i, h):
        for stage, lags in ((stage_b, LAGS_B), (stage_a, LAGS_A)):
            k = i - lags[h]

            @pl.when(jnp.logical_and(k >= 0, k < chunks))
            def _():
                l, m = owner(k)
                stage(h, l * shards + m)

    done = max(LAGS_A[-1], LAGS_B[-1])

    def step(i, _):
        for h in range(7):
            ring_steps(i, h)

        first = i - done

        @pl.when(jnp.logical_and(first >= 0, first < shards))
        def _():
            compute(0, first)

        second = first - LAG

        @pl.when(second >= shards)
        def _():
            compute(1, second)

        return 0

    lax.fori_loop(0, chunks + done + LAG, step, 0)

    part = jnp.sum(acc[...].T, axis=0, keepdims=True)
    RS[me] = part
    rs_copies = [
        remote(RS.at[me], RS.at[me], rss.at[i], rsr.at[me], mate(s)) for i, s in enumerate(mp_peers)
    ]
    for copy in rs_copies:
        copy.start()

    for i, s in enumerate(mp_peers):
        remote(RS.at[s], RS.at[s], rss.at[i], rsr.at[s], mate(s)).wait_recv()
    row = jnp.sum(RS[...], axis=0) / neur
    means[...] = row
    G[b] = jnp.broadcast_to(jnp.sum(row, axis=1, keepdims=True), (1, 128))

    def tell(d, _):
        to = lax.rem(b + d, NX * NZ) * shards + me
        remote(G.at[b], G.at[b], gs, gr, to).start()
        return 0

    lax.fori_loop(1, NX * NZ, tell, 0)
    others = G.at[pl.ds(0, NX * NZ - 1)]
    pltpu.make_async_copy(others, others, gr).wait()
    grand[...] = jnp.sum(G[...], axis=0) / rows_all
    for s in mp_peers:
        y_arrival(1, s)

    def drain(k, _):
        for copy in a_copies(k) + b_copies(k):
            copy().wait_send()
        return 0

    lax.fori_loop(0, chunks, drain, 0)
    for l in range(layers):
        for i, s in enumerate(order):
            part_a(l, i, s).wait_send()
            part_b(l, i, s).wait_send()
        for s in mp_peers:
            y_copy(l, s).wait_send()
    for i, s in enumerate(order):
        bias_to(i, s).wait_send()
    for copy in rs_copies:
        copy.wait_send()
    pltpu.make_async_copy(others, others, gs).wait()


def on_device(features, tiles, biases, in_block):
    layers, cb, fan, own_rows, side = tiles.shape
    rows = features.shape[0]
    shards = lax.axis_size("mp")
    groups = lax.axis_size("batch")
    per_chunk = cb // shards * fan
    chunks = layers * shards
    vmem = pl.BlockSpec(memory_space=pltpu.VMEM)
    hbm = pl.BlockSpec(memory_space=pltpu.HBM)
    dma = pltpu.SemaphoreType.DMA
    current, means, grand = pl.pallas_call(
        functools.partial(kernel, cb * shards * side, rows * groups),
        out_shape=(
            jax.ShapeDtypeStruct((rows, cb * side), BF16),
            jax.ShapeDtypeStruct((1, rows), F32),
            jax.ShapeDtypeStruct((1, 128), F32),
        ),
        in_specs=[hbm, hbm, hbm, hbm],
        out_specs=(vmem, vmem, vmem),
        scratch_shapes=[
            pltpu.VMEM((cb, rows, side), BF16),
            pltpu.VMEM((cb, rows, side), BF16),
            pltpu.VMEM((chunks, NZ, NX, TA, own_rows, side), BF16),
            pltpu.VMEM((chunks, NX, NZ, per_chunk - TA, own_rows, side), BF16),
            pltpu.VMEM((shards, layers, cb // shards * side), F32),
            pltpu.VMEM((shards, cb // shards, rows, side), BF16),
            pltpu.VMEM((shards, rows, cb // shards * side), BF16),
            pltpu.VMEM((rows, side), F32),
            pltpu.VMEM((shards, 1, 128), F32),
            pltpu.VMEM((NX * NZ, 1, 128), F32),
            pltpu.SMEM((fan, layers, shards * cb), jnp.int32),
            dma((layers, shards - 1, 2)),
            dma((chunks, 2)),
            dma((shards - 1,)),
            dma((shards,)),
            dma((chunks, 12)),
            dma((chunks, 12)),
            dma((chunks, 12)),
            dma((chunks, 12)),
            dma((layers, shards)),
            dma((layers, shards)),
            dma((shards - 1,)),
            dma((shards,)),
            dma,
            dma,
            dma,
            dma,
        ],
        compiler_params=pltpu.CompilerParams(
            collective_id=0, has_side_effects=True, vmem_limit_bytes=67043328
        ),
    )(
        jnp.transpose(in_block, (2, 0, 1)),
        features,
        tiles.reshape(layers, shards, per_chunk, own_rows, side),
        biases,
    )
    return current, means.reshape(rows), grand[0, 0]


def solution(mesh):
    placed = (P("batch", "mp"), P(None, "mp", None, "batch", None), P(None, "mp"), P())
    return jax.shard_map(
        on_device,
        mesh=mesh,
        in_specs=placed,
        out_specs=(P("batch", "mp"), P("batch"), P()),
        check_vma=False,
    )
```

time: 150 us -> 116 us (0.77)
  Pallas kernels: 142 us -> 111 us
  local copies, waits for them, and re-layouts: 5.96 us -> 3.62 us
    pallas_call x1, Pallas kernels: 142 us -> 111 us  [on_device(): pl.pallas_call(functools.partial(kernel, cb * shards * side, rows * group...]
    unnamed x10 -> x6, local copies, waits for them, and re-layouts: 5.96 us -> 3.62 us
where the time goes in v2:
time: 116 us
  Pallas kernels  111 us (96%)
  local copies, waits for them, and re-layouts  3.62 us (3%)
  between operations  1.82 us (2%)
    pallas_call x1, Pallas kernels, on_device(): pl.pallas_call(functools.partial(kernel, cb * shards * side, rows * group...  111 us
    unnamed x6, local copies, waits for them, and re-layouts  3.62 us

profile of v2, /device:TPU:1, one launch (start us, length us, event | category | flops | bytes accessed | tf_op | source)
XLA Modules:
  0.0 116.2 jit_solution(14438879709358706852)
XLA Ops:
  0.6 110.8 %shard_map.67 = (bf16[128,8192]{1,0:T(8,128)(2,1)}, f32[1,128]{1,0:T(1,128)}, f32[1,128]{1,0:T(1,128)}) custom-call(s32[3,2,512]{2,1,0:T(2,128)} %bitcast.6, bf16[128,8192]{1,0:T(8,128)(2,1)} %feat.1, bf16[2,8,24,4,128]{4,3,2,1,0:T(4,128)(2,1)} %bitcast.5, f32[2,8192]{1,0:T(2,128)} %bias.1), custom_call_target="tpu_custom_call" | custom-call | tf_op jit(solution)/shard_map/pallas_call | solution.py:373
  111.4 0.0 copy-start.1
  111.4 0.0 copy-start
  111.4 3.1 %copy.10 = bf16[128,8192]{1,0:T(8,128)(2,1)} copy(bf16[128,8192]{1,0:T(8,128)(2,1)} %get-tuple-element.12) | data formatting | bytes 4194304
  114.5 0.0 copy-done.1
  114.5 0.5 copy.11
  115.1 0.0 copy-done
Async XLA Ops:
  111.4 3.1 %copy-start.1 = (f32[1,128]{1,0:T(1,128)S(1)}, f32[1,128]{1,0:T(1,128)}, u32[]{:S(2)}) copy-start(f32[1,128]{1,0:T(1,128)} %get-tuple-element.7) | copy-start | bytes 1540
  111.4 3.6 %copy-start = (f32[1,128]{1,0:T(1,128)S(1)}, f32[1,128]{1,0:T(1,128)}, u32[]{:S(2)}) copy-start(f32[1,128]{1,0:T(1,128)} %get-tuple-element.8) | copy-start | bytes 1540

commit v3 on v2

--- a/solution.py
+++ b/solution.py
@@ -12,7 +12,7 @@
 TA = 10
 LAGS_A = (0, 1, 2, 3, 4, 5, 6)
 LAGS_B = (0, 1, 2, 3, 4, 5, 6)
-LAG = 1
+HEAD = 0
 F32 = jnp.float32
 BF16 = jnp.bfloat16
 
@@ -22,7 +22,7 @@
     ib, feat, tiles, bias,
     out, means, grand,
     X0, X1, WA, WB, B, O0, O1, acc, RS, G, ids,
-    p0s, p0r, pbs, pbr, sA, rA, sB, rB, ys, yr, rss, rsr, gs, gr, fsem, isem,
+    p0s, p0r, pbs, pbr, sA, rA, sB, rB, ys, yr, rss, rsr, gs, gr, fsem, isem, osem,
 ):
     layers = tiles.shape[0]
     shards = tiles.shape[1]
@@ -42,7 +42,7 @@
     def device(xx, zz, s):
         return (xx * NZ + zz) * shards + s
 
-    near = {d: zat(d) for d in range(-3, 4)}
+    near = {d: zat(d) for d in range(-3, NZ // 2 + 1)}
     right, left = device(xr, z, me), device(xl, z, me)
     up, down = device(x, near[1], me), device(x, near[-1], me)
 
@@ -71,6 +71,8 @@
         return 0
 
     barrier = pltpu.get_barrier_semaphore()
+    across = device(lax.rem(x + NX // 2, NX), z, me)
+    beyond = {d: device(x, near[d], me) for d in near if d != 0}
     greeted = [mate(s) for s in mp_peers] + [right, left, up, down]
     for dev in greeted:
         pl.semaphore_signal(
@@ -126,8 +128,9 @@
     acc[...] = jnp.zeros_like(acc)
 
     def owner(k):
-        l = jnp.where(k >= shards, 1, 0)
-        n = lax.rem(k + (1 - l) * (shards - 1), shards)
+        tail = k >= shards + 1
+        l = jnp.where(jnp.logical_or(k == 1, tail), 1, 0)
+        n = jnp.where(k < 2, shards - 1, jnp.where(tail, k - (shards + 1), k - 2))
         dy = jnp.where(n < 2, 2, jnp.where(n < 6, 1 + 2 * lax.rem(n, 2), 0))
         dc = jnp.where(n < 2, n, jnp.where(n < 6, lax.div(n - 2, 2), 7 - n))
         return l, peer(dy, dc)
@@ -173,7 +176,7 @@
             go(WB.at[q, xr, half:NZ], 11, left),
         ]
 
-    def stage_a(h, q):
+    def stage_a(h, k, q):
         copies = a_copies(q)
 
         def forward(needs, starts):
@@ -189,6 +192,11 @@
             forward((0,), (2,))
             forward((1,), (3,))
         elif h == 2:
+
+            @pl.when(k < HEAD)
+            def _():
+                forward((0, 1), ())
+
             forward((2, 3), (4, 5))
         elif h < 6:
             forward((2 * h - 2,), (2 * h,))
@@ -196,7 +204,7 @@
         else:
             forward((10, 11), ())
 
-    def stage_b(h, q):
+    def stage_b(h, k, q):
         copies = b_copies(q)
 
         def forward(needs, starts):
@@ -209,12 +217,41 @@
             pltpu.make_async_copy(WB.at[q, x, z], WB.at[q, x, z], p0r.at[q, 1]).wait()
             forward((), (0, 1))
         elif h == 4:
+
+            @pl.when(k < HEAD)
+            def _():
+                forward(range(6), ())
+
             forward((6, 7), (8, 9))
         elif h < 6:
             forward((2 * h - 2,), (2 * h,))
             forward((2 * h - 1,), (2 * h + 1,))
         else:
             forward((10, 11), ())
+
+    def head(k):
+        l, m = owner(k)
+        q = l * shards + m
+        tb = per_chunk - TA
+        cut_a, cut_b = TA // 2, tb // 2
+
+        def go_a(ref, i, dev):
+            remote(ref, ref, sA.at[q, i], rA.at[q, i], dev).start()
+
+        def go_b(ref, i, dev):
+            remote(ref, ref, sB.at[q, i], rB.at[q, i], dev).start()
+
+        pltpu.make_async_copy(WB.at[q, x, z], WB.at[q, x, z], p0r.at[q, 1]).wait()
+        for d in range(NZ // 2 - 1, 0, -1):
+            go_b(WB.at[q, x, z], 2 * d - 2, beyond[d])
+            go_b(WB.at[q, x, z], 2 * d - 1, beyond[-d])
+        go_b(WB.at[q, x, z, 0:cut_b], 6, beyond[NZ // 2])
+        go_b(WB.at[q, x, z, cut_b:tb], 7, beyond[NZ // 2])
+        pltpu.make_async_copy(WA.at[q, z, x], WA.at[q, z, x], p0r.at[q, 0]).wait()
+        go_a(WA.at[q, z, x, 0:cut_a], 2, across)
+        go_a(WA.at[q, z, x, cut_a:TA], 3, across)
+        go_a(WA.at[q, z, x], 0, right)
+        go_a(WA.at[q, z, x], 1, left)
 
     mine = pl.ds(me * cols, cols)
     mine_out = pl.ds(pl.multiple_of(me * cols * 128, 128), cols * 128)
@@ -248,7 +285,7 @@
             pltpu.make_async_copy(B.at[m], B.at[m], pbr.at[m]).wait()
         else:
 
-            @pl.when(k == shards)
+            @pl.when(k == 1)
             def _():
                 for s in mp_peers:
                     y_arrival(0, s)
@@ -278,42 +315,56 @@
             if l == 0:
                 X1[mine] = O0[m]
             else:
-                out[:, mine_out] = O1[m]
+                pltpu.make_async_copy(O1.at[me], out.at[:, mine_out], osem).start()
 
         @pl.when(m != me)
         def _():
             y_copy(l, m).start()
 
     def ring_steps(i, h):
-        for stage, lags in ((stage_b, LAGS_B), (stage_a, LAGS_A)):
-            k = i - lags[h]
-
-            @pl.when(jnp.logical_and(k >= 0, k < chunks))
+        for stage, lags, direct in ((stage_b, LAGS_B, 4), (stage_a, LAGS_A, 2)):
+            u = i - lags[h]
+            k = u + HEAD
+            valid = jnp.logical_and(u >= 0, k < chunks)
+            if h >= direct:
+                early = jnp.logical_and(u >= -direct, u < HEAD - direct)
+                k = jnp.where(u < HEAD - direct, u + direct, k)
+                valid = jnp.logical_or(valid, early)
+
+            @pl.when(valid)
             def _():
                 l, m = owner(k)
-                stage(h, l * shards + m)
-
-    done = max(LAGS_A[-1], LAGS_B[-1])
+                stage(h, k, l * shards + m)
+
+    done = max(LAGS_A[-1], LAGS_B[-1]) - HEAD
 
     def step(i, _):
         for h in range(7):
             ring_steps(i, h)
 
         first = i - done
-
-        @pl.when(jnp.logical_and(first >= 0, first < shards))
+        inner = jnp.logical_and(first >= 2, first <= shards)
+
+        @pl.when(jnp.logical_or(first == 0, inner))
         def _():
             compute(0, first)
 
-        second = first - LAG
-
-        @pl.when(second >= shards)
+        opening = first == shards + 1
+
+        def both(r, _):
+            own_first = jnp.logical_and(opening, r == 0)
+            compute(1, jnp.where(own_first, 1, first))
+            return 0
+
+        @pl.when(first > shards)
         def _():
-            compute(1, second)
+            lax.fori_loop(0, jnp.where(opening, 2, 1), both, 0)
 
         return 0
 
-    lax.fori_loop(0, chunks + done + LAG, step, 0)
+    for k in range(HEAD):
+        head(jnp.int32(k))
+    lax.fori_loop(0, chunks + done, step, 0)
 
     part = jnp.sum(acc[...].T, axis=0, keepdims=True)
     RS[me] = part
@@ -323,6 +374,12 @@
     for copy in rs_copies:
         copy.start()
 
+    def drain(k, _):
+        for copy in a_copies(k) + b_copies(k):
+            copy().wait_send()
+        return 0
+
+    lax.fori_loop(0, chunks, drain, 0)
     for i, s in enumerate(mp_peers):
         remote(RS.at[s], RS.at[s], rss.at[i], rsr.at[s], mate(s)).wait_recv()
     row = jnp.sum(RS[...], axis=0) / neur
@@ -335,18 +392,6 @@
         return 0
 
     lax.fori_loop(1, NX * NZ, tell, 0)
-    others = G.at[pl.ds(0, NX * NZ - 1)]
-    pltpu.make_async_copy(others, others, gr).wait()
-    grand[...] = jnp.sum(G[...], axis=0) / rows_all
-    for s in mp_peers:
-        y_arrival(1, s)
-
-    def drain(k, _):
-        for copy in a_copies(k) + b_copies(k):
-            copy().wait_send()
-        return 0
-
-    lax.fori_loop(0, chunks, drain, 0)
     for l in range(layers):
         for i, s in enumerate(order):
             part_a(l, i, s).wait_send()
@@ -357,6 +402,12 @@
         bias_to(i, s).wait_send()
     for copy in rs_copies:
         copy.wait_send()
+    for s in mp_peers:
+        y_arrival(1, s)
+    pltpu.make_async_copy(O1.at[me], out.at[:, mine_out], osem).wait()
+    others = G.at[pl.ds(0, NX * NZ - 1)]
+    pltpu.make_async_copy(others, others, gr).wait()
+    grand[...] = jnp.sum(G[...], axis=0) / rows_all
     pltpu.make_async_copy(others, others, gs).wait()
 
 
@@ -407,15 +458,21 @@
             dma,
             dma,
             dma,
+            dma,
         ],
         compiler_params=pltpu.CompilerParams(
-            collective_id=0, has_side_effects=True, vmem_limit_bytes=67043328
+            collective_id=0, has_side_effects=True, vmem_limit_bytes=48 * 1024 * 1024
         ),
     )(
-        jnp.transpose(in_block, (2, 0, 1)),
-        features,
-        tiles.reshape(layers, shards, per_chunk, own_rows, side),
-        biases,
+        *(
+            pltpu.with_memory_space_constraint(v, pltpu.HBM)
+            for v in (
+                jnp.transpose(in_block, (2, 0, 1)),
+                features,
+                tiles.reshape(layers, shards, per_chunk, own_rows, side),
+                biases,
+            )
+        )
     )
     return current, means.reshape(rows), grand[0, 0]
 

time: 116 us -> 111 us (0.957)
  Pallas kernels: 111 us -> 107 us
  local copies, waits for them, and re-layouts: 3.62 us -> 1.83 us
    pallas_call x1, Pallas kernels: 111 us -> 107 us  [on_device(): pl.pallas_call(functools.partial(kernel, cb * shards * side, rows * group...]
    unnamed x6 -> x2, local copies, waits for them, and re-layouts: 3.62 us -> 1.83 us
where the time goes in v3:
time: 111 us
  Pallas kernels  107 us (96%)
  local copies, waits for them, and re-layouts  1.83 us (2%)
  between operations  1.81 us (2%)
    pallas_call x1, Pallas kernels, on_device(): pl.pallas_call(functools.partial(kernel, cb * shards * side, rows * group...  107 us

profile of v3, /device:TPU:1, one launch (start us, length us, event | category | flops | bytes accessed | tf_op | source)
XLA Modules:
  0.0 110.9 jit_solution(10725423883649548838)
XLA Ops:
  0.6 107.2 %shard_map.67 = (bf16[128,8192]{1,0:T(8,128)(2,1)S(1)}, f32[1,128]{1,0:T(1,128)S(1)}, f32[1,128]{1,0:T(1,128)S(1)}) custom-call(s32[3,2,512]{2,1,0:T(2,128)} %bitcast.8, bf16[128,8192]{1,0:T(8,128)(2,1)} %feat.1, bf16[2,8,24,4,128]{4,3,2,1,0:T(4,128)(2,1)} %bitcast.7, f32[2,8192]{1,0:T(2,128)} %bias.1), custom_call_target="tpu_custom_call" | custom-call | tf_op jit(solution)/shard_map/pallas_call | solution.py:424
  107.9 1.3 %copy.10 = bf16[128,8192]{1,0:T(8,128)(2,1)} copy(bf16[128,8192]{1,0:T(8,128)(2,1)S(1)} %get-tuple-element.12) | data formatting | bytes 4194304
  109.2 0.5 copy.11

commit v4 on v3

--- a/solution.py
+++ b/solution.py
@@ -12,7 +12,7 @@
 TA = 10
 LAGS_A = (0, 1, 2, 3, 4, 5, 6)
 LAGS_B = (0, 1, 2, 3, 4, 5, 6)
-HEAD = 0
+SLOTS = 5
 F32 = jnp.float32
 BF16 = jnp.bfloat16
 
@@ -42,7 +42,7 @@
     def device(xx, zz, s):
         return (xx * NZ + zz) * shards + s
 
-    near = {d: zat(d) for d in range(-3, NZ // 2 + 1)}
+    near = {d: zat(d) for d in range(-3, 4)}
     right, left = device(xr, z, me), device(xl, z, me)
     up, down = device(x, near[1], me), device(x, near[-1], me)
 
@@ -71,8 +71,6 @@
         return 0
 
     barrier = pltpu.get_barrier_semaphore()
-    across = device(lax.rem(x + NX // 2, NX), z, me)
-    beyond = {d: device(x, near[d], me) for d in near if d != 0}
     greeted = [mate(s) for s in mp_peers] + [right, left, up, down]
     for dev in greeted:
         pl.semaphore_signal(
@@ -135,9 +133,11 @@
         dc = jnp.where(n < 2, n, jnp.where(n < 6, lax.div(n - 2, 2), 7 - n))
         return l, peer(dy, dc)
 
-    def a_copies(q):
+    def a_copies(q, k):
+        slot = lax.rem(k, SLOTS)
+
         def go(ref, i, dev):
-            return lambda: remote(ref, ref, sA.at[q, i], rA.at[q, i], dev)
+            return lambda: remote(ref, ref, sA.at[slot, i], rA.at[slot, i], dev)
 
         half, cut = NX // 2, TA // 2
         return [
@@ -155,9 +155,11 @@
             go(WA.at[q, near[3], half:NX], 11, down),
         ]
 
-    def b_copies(q):
+    def b_copies(q, k):
+        slot = lax.rem(k, SLOTS)
+
         def go(ref, i, dev):
-            return lambda: remote(ref, ref, sB.at[q, i], rB.at[q, i], dev)
+            return lambda: remote(ref, ref, sB.at[slot, i], rB.at[slot, i], dev)
 
         tb = per_chunk - TA
         half, cut = NZ // 2, tb // 2
@@ -177,11 +179,18 @@
         ]
 
     def stage_a(h, k, q):
-        copies = a_copies(q)
+        copies = a_copies(q, k)
 
         def forward(needs, starts):
             for n in needs:
                 copies[n]().wait_recv()
+            if starts:
+
+                @pl.when(k >= SLOTS)
+                def _():
+                    for n in starts:
+                        copies[n]().wait_send()
+
             for n in starts:
                 copies[n]().start()
 
@@ -192,11 +201,6 @@
             forward((0,), (2,))
             forward((1,), (3,))
         elif h == 2:
-
-            @pl.when(k < HEAD)
-            def _():
-                forward((0, 1), ())
-
             forward((2, 3), (4, 5))
         elif h < 6:
             forward((2 * h - 2,), (2 * h,))
@@ -205,11 +209,18 @@
             forward((10, 11), ())
 
     def stage_b(h, k, q):
-        copies = b_copies(q)
+        copies = b_copies(q, k)
 
         def forward(needs, starts):
             for n in needs:
                 copies[n]().wait_recv()
+            if starts:
+
+                @pl.when(k >= SLOTS)
+                def _():
+                    for n in starts:
+                        copies[n]().wait_send()
+
             for n in starts:
                 copies[n]().start()
 
@@ -217,41 +228,12 @@
             pltpu.make_async_copy(WB.at[q, x, z], WB.at[q, x, z], p0r.at[q, 1]).wait()
             forward((), (0, 1))
         elif h == 4:
-
-            @pl.when(k < HEAD)
-            def _():
-                forward(range(6), ())
-
             forward((6, 7), (8, 9))
         elif h < 6:
             forward((2 * h - 2,), (2 * h,))
             forward((2 * h - 1,), (2 * h + 1,))
         else:
             forward((10, 11), ())
-
-    def head(k):
-        l, m = owner(k)
-        q = l * shards + m
-        tb = per_chunk - TA
-        cut_a, cut_b = TA // 2, tb // 2
-
-        def go_a(ref, i, dev):
-            remote(ref, ref, sA.at[q, i], rA.at[q, i], dev).start()
-
-        def go_b(ref, i, dev):
-            remote(ref, ref, sB.at[q, i], rB.at[q, i], dev).start()
-
-        pltpu.make_async_copy(WB.at[q, x, z], WB.at[q, x, z], p0r.at[q, 1]).wait()
-        for d in range(NZ // 2 - 1, 0, -1):
-            go_b(WB.at[q, x, z], 2 * d - 2, beyond[d])
-            go_b(WB.at[q, x, z], 2 * d - 1, beyond[-d])
-        go_b(WB.at[q, x, z, 0:cut_b], 6, beyond[NZ // 2])
-        go_b(WB.at[q, x, z, cut_b:tb], 7, beyond[NZ // 2])
-        pltpu.make_async_copy(WA.at[q, z, x], WA.at[q, z, x], p0r.at[q, 0]).wait()
-        go_a(WA.at[q, z, x, 0:cut_a], 2, across)
-        go_a(WA.at[q, z, x, cut_a:TA], 3, across)
-        go_a(WA.at[q, z, x], 0, right)
-        go_a(WA.at[q, z, x], 1, left)
 
     mine = pl.ds(me * cols, cols)
     mine_out = pl.ds(pl.multiple_of(me * cols * 128, 128), cols * 128)
@@ -322,21 +304,15 @@
             y_copy(l, m).start()
 
     def ring_steps(i, h):
-        for stage, lags, direct in ((stage_b, LAGS_B, 4), (stage_a, LAGS_A, 2)):
-            u = i - lags[h]
-            k = u + HEAD
-            valid = jnp.logical_and(u >= 0, k < chunks)
-            if h >= direct:
-                early = jnp.logical_and(u >= -direct, u < HEAD - direct)
-                k = jnp.where(u < HEAD - direct, u + direct, k)
-                valid = jnp.logical_or(valid, early)
-
-            @pl.when(valid)
+        for stage, lags in ((stage_b, LAGS_B), (stage_a, LAGS_A)):
+            k = i - lags[h]
+
+            @pl.when(jnp.logical_and(k >= 0, k < chunks))
             def _():
                 l, m = owner(k)
                 stage(h, k, l * shards + m)
 
-    done = max(LAGS_A[-1], LAGS_B[-1]) - HEAD
+    done = max(LAGS_A[-1], LAGS_B[-1])
 
     def step(i, _):
         for h in range(7):
@@ -362,8 +338,6 @@
 
         return 0
 
-    for k in range(HEAD):
-        head(jnp.int32(k))
     lax.fori_loop(0, chunks + done, step, 0)
 
     part = jnp.sum(acc[...].T, axis=0, keepdims=True)
@@ -375,11 +349,11 @@
         copy.start()
 
     def drain(k, _):
-        for copy in a_copies(k) + b_copies(k):
+        for copy in a_copies(k, k) + b_copies(k, k):
             copy().wait_send()
         return 0
 
-    lax.fori_loop(0, chunks, drain, 0)
+    lax.fori_loop(0, SLOTS, drain, 0)
     for i, s in enumerate(mp_peers):
         remote(RS.at[s], RS.at[s], rss.at[i], rsr.at[s], mate(s)).wait_recv()
     row = jnp.sum(RS[...], axis=0) / neur
@@ -446,10 +420,10 @@
             dma((chunks, 2)),
             dma((shards - 1,)),
             dma((shards,)),
-            dma((chunks, 12)),
-            dma((chunks, 12)),
-            dma((chunks, 12)),
-            dma((chunks, 12)),
+            dma((SLOTS, 12)),
+            dma((SLOTS, 12)),
+            dma((SLOTS, 12)),
+            dma((SLOTS, 12)),
             dma((layers, shards)),
             dma((layers, shards)),
             dma((shards - 1,)),

time: 111 us -> 106 us (0.955)
  Pallas kernels: 107 us -> 102 us
    pallas_call x1, Pallas kernels: 107 us -> 102 us  [on_device(): pl.pallas_call(functools.partial(kernel, cb * shards * side, rows * group...]
where the time goes in v4:
time: 106 us
  Pallas kernels  102 us (96%)
  local copies, waits for them, and re-layouts  1.83 us (2%)
  between operations  1.81 us (2%)
    pallas_call x1, Pallas kernels, on_device(): pl.pallas_call(functools.partial(kernel, cb * shards * side, rows * group...  102 us

profile of v4, /device:TPU:1, one launch (start us, length us, event | category | flops | bytes accessed | tf_op | source)
XLA Modules:
  0.0 106.1 jit_solution(1273683419232398622)
XLA Ops:
  0.6 102.4 %shard_map.67 = (bf16[128,8192]{1,0:T(8,128)(2,1)S(1)}, f32[1,128]{1,0:T(1,128)S(1)}, f32[1,128]{1,0:T(1,128)S(1)}) custom-call(s32[3,2,512]{2,1,0:T(2,128)} %bitcast.8, bf16[128,8192]{1,0:T(8,128)(2,1)} %feat.1, bf16[2,8,24,4,128]{4,3,2,1,0:T(4,128)(2,1)} %bitcast.7, f32[2,8192]{1,0:T(2,128)} %bias.1), custom_call_target="tpu_custom_call" | custom-call | tf_op jit(solution)/shard_map/pallas_call | solution.py:398
  103.1 1.3 %copy.10 = bf16[128,8192]{1,0:T(8,128)(2,1)} copy(bf16[128,8192]{1,0:T(8,128)(2,1)S(1)} %get-tuple-element.12) | data formatting | bytes 4194304
  104.4 0.5 copy.11

commit v5 on v4

--- a/solution.py
+++ b/solution.py
@@ -12,7 +12,7 @@
 TA = 10
 LAGS_A = (0, 1, 2, 3, 4, 5, 6)
 LAGS_B = (0, 1, 2, 3, 4, 5, 6)
-SLOTS = 5
+SLOTS = 4
 F32 = jnp.float32
 BF16 = jnp.bfloat16
 
@@ -101,18 +101,18 @@
     def part_a(l, i, s):
         q = l * shards + me
         return remote(
-            tiles.at[l, s, 0:TA], WA.at[q, z, x], p0s.at[l, i, 0], p0r.at[q, 0], mate(s)
+            tiles.at[l, s, 0:TA], WA.at[q, z, x], p0s, p0r.at[q, 0], mate(s)
         )
 
     def part_b(l, i, s):
         q = l * shards + me
         return remote(
-            tiles.at[l, s, TA:per_chunk], WB.at[q, x, z], p0s.at[l, i, 1], p0r.at[q, 1], mate(s)
+            tiles.at[l, s, TA:per_chunk], WB.at[q, x, z], p0s, p0r.at[q, 1], mate(s)
         )
 
     def bias_to(i, s):
         cut = pl.ds(pl.multiple_of(s * cols * 128, 128), cols * 128)
-        return remote(bias.at[:, cut], B.at[me], pbs.at[i], pbr.at[me], mate(s))
+        return remote(bias.at[:, cut], B.at[me], pbs, pbr.at[me], mate(s))
 
     order = [peer(NY - dy, dc) for dy, dc in offsets]
     for l in range(layers):
@@ -243,7 +243,7 @@
             src, dst = O0.at[m], X1.at[mine]
         else:
             src, dst = O1.at[m], out.at[:, mine_out]
-        return remote(src, dst, ys.at[l, m], yr.at[l, me], mate(m))
+        return remote(src, dst, ys.at[l], yr.at[l, me], mate(m))
 
     def y_arrival(l, s):
         if l == 0:
@@ -251,7 +251,7 @@
         else:
             cut = pl.ds(pl.multiple_of(s * cols * 128, 128), cols * 128)
             src, dst = O1.at[s], out.at[:, cut]
-        remote(src, dst, ys.at[l, s], yr.at[l, s], mate(s)).wait_recv()
+        remote(src, dst, ys.at[l], yr.at[l, s], mate(s)).wait_recv()
 
     def compute(l, k):
         _, m = owner(k)
@@ -343,7 +343,7 @@
     part = jnp.sum(acc[...].T, axis=0, keepdims=True)
     RS[me] = part
     rs_copies = [
-        remote(RS.at[me], RS.at[me], rss.at[i], rsr.at[me], mate(s)) for i, s in enumerate(mp_peers)
+        remote(RS.at[me], RS.at[me], rss, rsr.at[me], mate(s)) for i, s in enumerate(mp_peers)
     ]
     for copy in rs_copies:
         copy.start()
@@ -355,7 +355,7 @@
 
     lax.fori_loop(0, SLOTS, drain, 0)
     for i, s in enumerate(mp_peers):
-        remote(RS.at[s], RS.at[s], rss.at[i], rsr.at[s], mate(s)).wait_recv()
+        remote(RS.at[s], RS.at[s], rss, rsr.at[s], mate(s)).wait_recv()
     row = jnp.sum(RS[...], axis=0) / neur
     means[...] = row
     G[b] = jnp.broadcast_to(jnp.sum(row, axis=1, keepdims=True), (1, 128))
@@ -366,16 +366,16 @@
         return 0
 
     lax.fori_loop(1, NX * NZ, tell, 0)
-    for l in range(layers):
-        for i, s in enumerate(order):
-            part_a(l, i, s).wait_send()
-            part_b(l, i, s).wait_send()
-        for s in mp_peers:
-            y_copy(l, s).wait_send()
-    for i, s in enumerate(order):
-        bias_to(i, s).wait_send()
-    for copy in rs_copies:
-        copy.wait_send()
+    peers = pl.ds(0, shards - 1)
+    sent = (
+        (tiles.at[:, peers], p0s),
+        (bias.at[:, pl.ds(0, (shards - 1) * cols * 128)], pbs),
+        (O0.at[peers], ys.at[0]),
+        (O1.at[peers], ys.at[1]),
+        (RS.at[peers], rss),
+    )
+    for ref, sem in sent:
+        pltpu.make_async_copy(ref, ref, sem).wait()
     for s in mp_peers:
         y_arrival(1, s)
     pltpu.make_async_copy(O1.at[me], out.at[:, mine_out], osem).wait()
@@ -416,17 +416,17 @@
             pltpu.VMEM((shards, 1, 128), F32),
             pltpu.VMEM((NX * NZ, 1, 128), F32),
             pltpu.SMEM((fan, layers, shards * cb), jnp.int32),
-            dma((layers, shards - 1, 2)),
+            dma,
             dma((chunks, 2)),
-            dma((shards - 1,)),
+            dma,
             dma((shards,)),
             dma((SLOTS, 12)),
             dma((SLOTS, 12)),
             dma((SLOTS, 12)),
             dma((SLOTS, 12)),
+            dma((layers,)),
             dma((layers, shards)),
-            dma((layers, shards)),
-            dma((shards - 1,)),
+            dma,
             dma((shards,)),
             dma,
             dma,

time: 106 us -> 105 us (level)
  no operation moved by 1% of the time
where the time goes in v5:
time: 105 us
  Pallas kernels  102 us (97%)
  local copies, waits for them, and re-layouts  1.83 us (2%)
  between operations  1.81 us (2%)
    pallas_call x1, Pallas kernels, on_device(): pl.pallas_call(functools.partial(kernel, cb * shards * side, rows * group...  102 us

profile of v5, /device:TPU:1, one launch (start us, length us, event | category | flops | bytes accessed | tf_op | source)
XLA Modules:
  0.0 105.2 jit_solution(1574475156911635122)
XLA Ops:
  0.6 101.5 %shard_map.67 = (bf16[128,8192]{1,0:T(8,128)(2,1)S(1)}, f32[1,128]{1,0:T(1,128)S(1)}, f32[1,128]{1,0:T(1,128)S(1)}) custom-call(s32[3,2,512]{2,1,0:T(2,128)} %bitcast.8, bf16[128,8192]{1,0:T(8,128)(2,1)} %feat.1, bf16[2,8,24,4,128]{4,3,2,1,0:T(4,128)(2,1)} %bitcast.7, f32[2,8192]{1,0:T(2,128)} %bias.1), custom_call_target="tpu_custom_call" | custom-call | tf_op jit(solution)/shard_map/pallas_call | solution.py:398
  102.2 1.3 %copy.10 = bf16[128,8192]{1,0:T(8,128)(2,1)} copy(bf16[128,8192]{1,0:T(8,128)(2,1)S(1)} %get-tuple-element.12) | data formatting | bytes 4194304
  103.5 0.5 copy.11
